TPU v7x, 32 devices: a whole 2x2x4 slice. The times are simulated.
32 devices in a mesh: wide: 8 (over y, x, core), narrow: 4 (over z).
Axes of the slice: x: 2, y: 2, z: 4, core: 2. Of those that a mesh axis runs over, the one named last changes fastest.
Arguments:
- momentum: float32 [9216, 9216], P('wide', 'narrow'), may hold values from -3 to 3
- gradient: bfloat16 [9216, 9216], P('wide', 'narrow'), may hold values from -48 to 48
- right_factor: float32 [512, 9216], P('wide', 'narrow'), may hold values from -6 to 6
Outputs:
- new_momentum: float32 [9216, 9216], P('wide', 'narrow')
- new_right: float32 [512, 9216], P('wide', 'narrow')
- update: bfloat16 [9216, 9216], P('wide', 'narrow')
All inputs are finite; a program needn't handle non-finite values.
Results may differ from a plain program's by a relative error of at most 0.001.
Values sent between devices are 32-bit elements; how exact they have to be, the bound alone decides.
No kernel may reach another device: no remote copies, remote signals or barrier semaphores. Data moves between devices by JAX's collectives and lax.ppermute only.
A program may use at most 128 MiB of HBM per device.

v0:
```python
import jax
import jax.numpy as jnp
from jax import lax
from jax.sharding import PartitionSpec as P

N_COLS = 9216
EPS = 1e-06
MU = 0.95


def orthonormal(projected, gram_matrix):
    factor_lower = jnp.linalg.cholesky(gram_matrix)
    return jax.scipy.linalg.solve_triangular(factor_lower, projected.T, lower=True).T


def matmul(left, right):
    return jnp.dot(left, right, preferred_element_type=jnp.float32, precision=lax.Precision.HIGHEST)


def per_device(momentum, gradient, right_factor):
    blended = momentum + gradient.astype(jnp.float32)
    partial_left = matmul(blended, lax.all_gather(right_factor, "wide", axis=0, tiled=True).T)
    projected = lax.psum(partial_left, "narrow")
    gram_matrix = lax.psum(matmul(projected.T, projected), "wide")
    left_basis = orthonormal(projected, gram_matrix)
    columns = left_basis
    right_block = lax.psum_scatter(
        matmul(columns.T, blended), "wide", scatter_dimension=0, tiled=True
    )
    squares = lax.psum(jnp.sum(right_block * right_block, axis=1), "narrow")
    root_mean = jnp.sqrt(squares / N_COLS + EPS)
    new_right = right_block / root_mean[:, None]
    pieces = (
        lax.all_gather(right_block, "wide", axis=0, tiled=True),
        lax.all_gather(root_mean, "wide", axis=0, tiled=True),
    )
    columns = left_basis
    normed = pieces[0] / pieces[1][:, None]
    feedback = matmul(columns, pieces[0])
    direction = matmul(columns, normed)
    new_momentum = blended - (1.0 - MU) * feedback
    return (new_momentum, new_right, direction.astype(jnp.bfloat16))


def solution(mesh):
    return jax.shard_map(
        per_device,
        mesh=mesh,
        in_specs=(P("wide", "narrow"), P("wide", "narrow"), P("wide", "narrow")),
        out_specs=(P("wide", "narrow"), P("wide", "narrow"), P("wide", "narrow")),
        check_vma=False,
    )
```

profile of v0, /device:TPU:0, one launch (start us, length us, event | category | flops | bytes accessed | tf_op | source)
XLA Modules:
  0.0 566.0 jit_solution(15770033689719844626)
XLA Ops:
  7.2 0.7 all-gather.3.cloned.1.call-update
  7.9 43.5 %all-gather.3.cloned.1.call-done = f32[512,2304]{1,0:T(8,128)} async-done(((f32[64,2304]{1,0:T(8,128)}), f32[512,2304]{1,0:T(8,128)}) %all-gather.3.cloned.1.call-update) | async-done | bytes 4718608 | tf_op jit(solution)/shard_map/all_gather | solution.py:22
  51.4 22.9 %fusion.3 = f32[1152,512]{1,0:T(8,128)} fusion(f32[512,2304]{1,0:T(8,128)} %all-gather.3.cloned.1.call-done, f32[1152,2304]{1,0:T(8,128)} %param.3, bf16[1152,2304]{1,0:T(8,128)(2,1)} %param.4), kind=kOutput, calls=%fused_computation.8 | convolution fusion | flops 16312762368 | bytes 23003136 | tf_op jit(solution)/shard_map/dot_general | solution.py:17
  74.4 94.7 %all-reduce.5.cloned.1.call-done = f32[1152,512]{1,0:T(8,128)} async-done(((f32[1152,512]{1,0:T(8,128)}), f32[1152,512]{1,0:T(8,128)}) %all-reduce.5.cloned.1.call-update) | async-done | bytes 2359312 | tf_op jit(solution)/shard_map/psum | solution.py:23
  169.1 7.7 %fusion.40 = f32[512,512]{0,1:T(8,128)} fusion(f32[1152,512]{1,0:T(8,128)} %all-reduce.5.cloned.1.call-done), kind=kOutput, calls=%fused_computation.82 | convolution fusion | flops 3623878656 | bytes 3407872 | tf_op jit(solution)/shard_map/dot_general | solution.py:17
  177.1 55.6 %all-reduce.7.cloned.1.call-done = f32[512,512]{0,1:T(8,128)} async-done(((f32[512,512]{0,1:T(8,128)}), f32[512,512]{0,1:T(8,128)}) %all-reduce.7.cloned.1.call-update) | async-done | bytes 1048592 | tf_op jit(solution)/shard_map/psum | solution.py:24
  232.7 1.6 copy.7
  234.6 1.0 copy-done.5
  235.6 11.7 %cholesky.104 = f32[128,128]{1,0:T(8,128)S(1)} custom-call(f32[128,128]{1,0:T(8,128)S(1)} %cholesky.266), custom_call_target="Cholesky" | custom-call | tf_op jit(solution)/shard_map/jit(cholesky)/cholesky | solution.py:12
  247.3 9.8 %custom-call.31 = f32[1,128,128]{1,2,0:T(8,128)S(1)} custom-call(f32[1,128,128]{2,1,0:T(8,128)S(1)} %get-tuple-element.30), custom_call_target="InvertDiagBlocksLowerTriangular" | custom-call | tf_op jit(solution)/shard_map/jit(cholesky)/cholesky | solution.py:12
  257.2 1.2 constant_dynamic-update-slice_fusion.3
  258.5 1.3 convolution_subtract_fusion.3
  259.8 11.7 %cholesky.217 = f32[128,128]{1,0:T(8,128)S(1)} custom-call(f32[128,128]{1,0:T(8,128)S(1)} %cholesky.270), custom_call_target="Cholesky" | custom-call | tf_op jit(solution)/shard_map/jit(cholesky)/cholesky | solution.py:12
  271.5 10.2 %custom-call.32 = f32[1,128,128]{1,2,0:T(8,128)S(1)} custom-call(f32[1,128,128]{2,1,0:T(8,128)S(1)} %get-tuple-element.27), custom_call_target="InvertDiagBlocksLowerTriangular" | custom-call | tf_op jit(solution)/shard_map/jit(cholesky)/cholesky | solution.py:12
  282.0 1.4 convolution_subtract_fusion.4
  283.4 0.6 cholesky.275
  284.1 13.2 %cholesky.238 = f32[128,128]{1,0:T(8,128)} custom-call(f32[128,128]{1,0:T(8,128)} %cholesky.275), custom_call_target="Cholesky" | custom-call | tf_op jit(solution)/shard_map/jit(cholesky)/cholesky | solution.py:12
  297.2 1.5 select_reduce_fusion.1
  298.7 0.7 compare_reduce_fusion.1
  299.4 11.3 %custom-call.33 = f32[1,128,128]{1,2,0:T(8,128)} custom-call(f32[1,128,128]{2,1,0:T(8,128)} %get-tuple-element.24), custom_call_target="InvertDiagBlocksLowerTriangular" | custom-call | tf_op jit(solution)/shard_map/jit(cholesky)/cholesky | solution.py:12
  310.7 1.0 convolution_dynamic-update-slice_fusion.1
  311.8 1.2 convolution_subtract_fusion.5
  313.0 11.7 %cholesky.255 = f32[128,128]{1,0:T(8,128)S(1)} custom-call(f32[128,128]{1,0:T(8,128)S(1)} %convolution_subtract_fusion.5), custom_call_target="Cholesky" | custom-call | tf_op jit(solution)/shard_map/jit(cholesky)/cholesky | solution.py:12
  324.7 0.6 compare_reduce_fusion
  325.4 0.6 compare_reduce_fusion.2
  328.5 1.3 select_select_fusion
  329.8 13.7 %while.1 = (s32[]{:T(128)}, f32[512,512]{1,0:T(8,128)}, s32[4,2]{0,1:T(2,128)S(1)}, f32[4,128,128]{2,1,0:T(8,128)}, s32[]{:T(128)}) while((s32[]{:T(128)}, f32[512,512]{1,0:T(8,128)}, s32[4,2]{0,1:T(2,128)S(1)}, f32[4,128,128]{2,1,0:T(8,128)}, s32[]{:T(128)}) %tuple.32), condition=%wide.while_cond, body=%wide.while_body.sunk | while | flops 2 | bytes 132205 | solution.py:13
  330.4 2.8 bitcast_dynamic-update-slice_fusion.2
  333.8 2.8 bitcast_dynamic-update-slice_fusion.2
  337.3 2.8 bitcast_dynamic-update-slice_fusion.2
  340.7 2.8 bitcast_dynamic-update-slice_fusion.2
  343.5 40.1 %custom-call.34 = f32[4,128,128]{1,2,0:T(8,128)S(1)} custom-call(f32[4,128,128]{2,1,0:T(8,128)} %get-tuple-element.10), custom_call_target="InvertDiagBlocksLowerTriangular" | custom-call | tf_op jit(solution)/shard_map/jit(_solve_triangular)/triangular_solve | solution.py:13
  383.6 0.7 fusion.14
  384.4 2.4 convolution_subtract_fusion.2
  386.8 1.6 fusion.27
  388.4 3.0 convolution_subtract_fusion.1
  391.5 0.7 fusion.25
  392.2 4.2 convolution_subtract_fusion
  396.5 0.7 fusion.24
  397.3 23.1 %fusion.2 = f32[512,2304]{1,0:T(8,128)} fusion(f32[1152,2304]{1,0:T(8,128)} %param.3, bf16[1152,2304]{1,0:T(8,128)(2,1)S(1)} %bitcast.55, f32[128,1152]{1,0:T(8,128)S(1)} %fusion.24, f32[128,1152]{1,0:T(8,128)S(1)} %fusion.25, f32[128,1152]{1,0:T(8,128)S(1)} %fusion.27, f32[128,1152]{1,0:T(8,128)S(1)} %fusion.14), kind=kOutput, calls=%fused_computation.7 | convolution fusion | flops 16314531840 | bytes 23003136 | tf_op jit(solution)/shard_map/dot_general | solution.py:17
  420.4 53.1 %reduce-scatter.2.cloned.1.call-done = f32[64,2304]{1,0:T(8,128)} async-done(((f32[512,2304]{1,0:T(8,128)}), f32[64,2304]{1,0:T(8,128)}) %reduce-scatter.2.cloned.1.call-update) | async-done | bytes 589840 | tf_op jit(solution)/shard_map/reduce_scatter | solution.py:27
  474.8 1.2 multiply_reduce_fusion
  476.0 11.7 %psum.23 = f32[64]{0:T(128)S(1)} all-reduce(f32[64]{0:T(128)S(1)} %multiply_reduce_fusion), channel_id=1, replica_groups=mesh['wide'=8,'narrow'=4] {'narrow'}, use_global_device_ids=true, to_apply=%region_12.13 | all-reduce | flops 64 | bytes 512 | tf_op jit(solution)/shard_map/psum | solution.py:30
  487.8 12.1 %all-reduce.1 = f32[512]{0:T(512)S(1)} all-reduce(f32[512]{0:T(512)S(1)} %get-tuple-element.31), channel_id=1, replica_groups=mesh['wide'=8,'narrow'=4] {'wide'}, use_global_device_ids=true, to_apply=%add.1 | all-reduce | flops 512 | bytes 4096
  499.9 2.0 broadcast_divide_fusion
  501.9 12.3 %all-gather.5.cloned.1.call-done = f32[512,2304]{1,0:T(8,128)} async-done(((f32[64,2304]{1,0:T(8,128)}), f32[512,2304]{1,0:T(8,128)}) %all-gather.5.cloned.1.call-update) | async-done | bytes 4718608 | tf_op jit(solution)/shard_map/all_gather | solution.py:34
  514.2 24.1 %fusion = f32[1152,2304]{1,0:T(8,128)} fusion(f32[512,2304]{1,0:T(8,128)} %all-gather.5.cloned.1.call-done, f32[1152,2304]{1,0:T(8,128)} %param.3, bf16[1152,2304]{1,0:T(8,128)(2,1)} %param.4, f32[128,1152]{1,0:T(8,128)S(1)} %fusion.24, f32[128,1152]{1,0:T(8,128)S(1)} %copy-done.2, f32[128,1152]{1,0:T(8,128)S(1)} %fusion.27, f32[128,1152]{1,0:T(8,128)S(1)} %fusion.14), kind=kOutput, calls=%fused_computation.3 | convolution fusion | flops 16319840256 | bytes 33619968 | tf_op jit(solution)/shard_map/dot_general | solution.py:17
  538.3 20.7 %convolution_convert_fusion = bf16[1152,2304]{1,0:T(8,128)(2,1)} fusion(f32[512,2304]{1,0:T(8,128)S(1)} %copy-done.3, f32[512]{0:T(512)S(1)} %all-reduce.1, f32[128,1152]{1,0:T(8,128)S(1)} %fusion.24, f32[128,1152]{1,0:T(8,128)S(1)} %copy-done.2, f32[128,1152]{1,0:T(8,128)S(1)} %fusion.27, f32[128,1152]{1,0:T(8,128)S(1)} %fusion.14), kind=kOutput, calls=%fused_computation.4 | convolution fusion | flops 16313057280 | bytes 12388352 | tf_op jit(solution)/shard_map/dot_general | solution.py:17
  (53 shorter events, 4.3 us)
Async XLA Ops:
  7.2 44.2 %all-gather.3.cloned.1.call-start = ((), (), s32[]{:S(2)}) async-start(), calls=%async_computation.1 | async-start | bytes 5308416 | tf_op jit(solution)/shard_map/all_gather | solution.py:22
  7.9 161.2 %all-reduce.5.cloned.1.call-start = ((), (), s32[]{:S(2)}) async-start(), calls=%async_computation.2 | async-start | bytes 4718592 | tf_op jit(solution)/shard_map/psum | solution.py:23
  74.3 158.4 %all-reduce.7.cloned.1.call-start = ((), (), s32[]{:S(2)}) async-start(), calls=%async_computation.3 | async-start | bytes 2097152 | tf_op jit(solution)/shard_map/psum | solution.py:24
  176.8 296.7 %reduce-scatter.2.cloned.1.call-start = ((), (), s32[]{:S(2)}) async-start(), calls=%async_computation.4 | async-start | bytes 5308416 | tf_op jit(solution)/shard_map/reduce_scatter | solution.py:27
  232.7 1.7 copy-start.4
  234.6 1.0 copy-start.5
  282.0 101.6 %copy-start = (f32[1152,512]{1,0:T(8,128)S(1)}, f32[1152,512]{1,0:T(8,128)}, u32[]{:S(2)}) copy-start(f32[1152,512]{1,0:T(8,128)} %all-reduce.5.cloned.1.call-done) | copy-start | bytes 7077892
  383.6 0.8 copy-start.6
  383.6 13.6 %slice-start = ((s8[5308416]{0:T(1024)(128)(4,1)}), s8[4194304]{0:T(1024)(128)(4,1)S(1)}, s32[]{:S(2)}) async-start(s8[5308416]{0:T(1024)(128)(4,1)} %bitcast.54), calls=%async_computation.6 | async-start | bytes 8388608
  386.8 4.7 copy-start.7
  388.4 8.8 %slice-start.1 = ((s8[5308416]{0:T(1024)(128)(4,1)}), s8[1114112]{0:T(1024)(128)(4,1)S(1)}, s32[]{:S(2)}) async-start(s8[5308416]{0:T(1024)(128)(4,1)} %bitcast.54), calls=%async_computation.7 | async-start | bytes 2228224
  392.2 5.0 copy-start.1
  420.3 53.2 %copy-start.8 = (u32[32]{0:T(128)S(1)}, u32[32]{0:T(128)}, u32[]{:S(2)}) copy-start(u32[32]{0:T(128)} %constant.172) | copy-start | bytes 388
  420.4 93.8 %copy-start.2 = (f32[128,1152]{1,0:T(8,128)S(1)}, f32[128,1152]{1,0:T(8,128)}, u32[]{:S(2)}) copy-start(f32[128,1152]{1,0:T(8,128)} %copy-done.1) | copy-start | bytes 1769476
  420.4 93.8 %all-gather.5.cloned.1.call-start = ((), (), s32[]{:S(2)}) async-start(), calls=%async_computation.5 | async-start | bytes 5308416 | tf_op jit(solution)/shard_map/all_gather | solution.py:34
  514.2 24.1 %copy-start.3 = (f32[512,2304]{1,0:T(8,128)S(1)}, f32[512,2304]{1,0:T(8,128)}, u32[]{:S(2)}) copy-start(f32[512,2304]{1,0:T(8,128)} %all-gather.5.cloned.1.call-done) | copy-start | bytes 14155780
Sparse Core Ops, SparseCore 0:
  9.9 41.4 all-gather.2
  74.4 94.6 all-reduce.4
  176.9 55.7 all-reduce.6
  420.5 53.0 reduce-scatter.1
  475.3 38.9 all-gather.4
where the time goes:
time: 574 us; the launch traced here: 566 us
  waiting for transfers between devices  260 us (45%)
  other arithmetic  128 us (22%)
  matrix products  118 us (21%)
  blocking collectives  23.8 us (4%)
  between operations  17.8 us (3%)
  local copies, waits for them, and re-layouts  17.7 us (3%)
    dot_general x5, matrix products, matmul(): jnp.dot(left, right, preferred_element_type=jnp.float32, precision=lax.Pr...  98.4 us
    psum x1, waiting for transfers between devices, per_device(): projected = lax.psum(partial_left, 'narrow')  94.7 us
    another operation x14, other arithmetic, orthonormal(): factor_lower = jnp.linalg.cholesky(gram_matrix)  83.1 us
    psum x1, waiting for transfers between devices, per_device(): gram_matrix = lax.psum(matmul(projected.T, projected), 'wide')  55.6 us
    reduce_scatter x1, waiting for transfers between devices, per_device(): lax.psum_scatter(matmul(columns.T, blended), 'wide', scatter_dimension=0,...  53.1 us
    all_gather x1, waiting for transfers between devices, per_device(): lax.all_gather(right_factor, 'wide', axis=0, tiled=True)  43.5 us
    another operation x3, other arithmetic, orthonormal(): jax.scipy.linalg.solve_triangular(factor_lower, projected.T, lower=True)  41.4 us
    another operation x12, local copies, waits for them, and re-layouts  13.7 us
  transfers between devices with their start and end apart: 5, of which 5 were waited for; matrix products, arithmetic and copies ran while one was open for 1% of the time, Pallas kernels for 0%

commit v1 on v0

--- a/solution.py
+++ b/solution.py
@@ -18,9 +18,19 @@
 
 
 def per_device(momentum, gradient, right_factor):
+
+    def form_turns_on_mesh(base_x):
+        net_axis = "narrow"
+        axis_n = lax.axis_size(net_axis)
+        r1 = lambda k_now: [(rr, rr ^ k_now) for rr in range(axis_n)]
+        piece_now = base_x
+        for m in range(axis_n.bit_length() - 1):
+            piece_now = piece_now + lax.ppermute(piece_now, net_axis, r1(1 << m))
+        return piece_now
+
     blended = momentum + gradient.astype(jnp.float32)
     partial_left = matmul(blended, lax.all_gather(right_factor, "wide", axis=0, tiled=True).T)
-    projected = lax.psum(partial_left, "narrow")
+    projected = form_turns_on_mesh(partial_left)
     gram_matrix = lax.psum(matmul(projected.T, projected), "wide")
     left_basis = orthonormal(projected, gram_matrix)
     columns = left_basis

time: 574 us -> 621 us (1.082)
  waiting for transfers between devices: 260 us -> 316 us
  matrix products: 118 us -> 111 us
    ppermute x0 -> x2, waiting for transfers between devices: none -> 154 us  [form_turns_on_mesh(): piece_now = piece_now + lax.ppermute(piece_now, net_axis, r1(1 << m))]
    psum x1 -> x0, waiting for transfers between devices: 94.7 us -> none  [per_device(): projected = lax.psum(partial_left, 'narrow')]
  transfers between devices with their start and end apart: 5 -> 6, of which waited for: 5 -> 6; matrix products, arithmetic and copies ran while one was open for 1% -> 1% of each run, Pallas kernels for 0% -> 0%
where the time goes in v1:
time: 621 us; the launch traced here: 613 us
  waiting for transfers between devices  316 us (51%)
  other arithmetic  127 us (20%)
  matrix products  111 us (18%)
  blocking collectives  23.8 us (4%)
  between operations  17.8 us (3%)
  local copies, waits for them, and re-layouts  13.3 us (2%)
    ppermute x2, waiting for transfers between devices, form_turns_on_mesh(): piece_now = piece_now + lax.ppermute(piece_now, net_axis, r1(1 << m))  154 us
    dot_general x5, matrix products, matmul(): jnp.dot(left, right, preferred_element_type=jnp.float32, precision=lax.Pr...  96.5 us
    another operation x14, other arithmetic, orthonormal(): factor_lower = jnp.linalg.cholesky(gram_matrix)  79 us
    reduce_scatter x1, waiting for transfers between devices, per_device(): lax.psum_scatter(matmul(columns.T, blended), 'wide', scatter_dimension=0,...  53.1 us
    psum x1, waiting for transfers between devices, per_device(): gram_matrix = lax.psum(matmul(projected.T, projected), 'wide')  53 us
    all_gather x1, waiting for transfers between devices, per_device(): lax.all_gather(right_factor, 'wide', axis=0, tiled=True)  43.5 us
    another operation x3, other arithmetic, orthonormal(): jax.scipy.linalg.solve_triangular(factor_lower, projected.T, lower=True)  40.3 us
  transfers between devices with their start and end apart: 6, of which 6 were waited for; matrix products, arithmetic and copies ran while one was open for 1% of the time, Pallas kernels for 0%

profile of v1, /device:TPU:0, one launch (start us, length us, event | category | flops | bytes accessed | tf_op | source)
XLA Modules:
  0.0 613.0 jit_solution(15405814856366141634)
XLA Ops:
  7.2 0.7 all-gather.3.cloned.1.call-update
  7.9 43.5 %all-gather.3.cloned.1.call-done = f32[512,2304]{1,0:T(8,128)} async-done(((f32[64,2304]{1,0:T(8,128)}), f32[512,2304]{1,0:T(8,128)}) %all-gather.3.cloned.1.call-update) | async-done | bytes 4718608 | tf_op jit(solution)/shard_map/all_gather | solution.py:32
  51.4 20.9 %fusion.3 = f32[1152,512]{1,0:T(8,128)S(1)} fusion(f32[512,2304]{1,0:T(8,128)} %all-gather.3.cloned.1.call-done, f32[1152,2304]{1,0:T(8,128)} %param.3, bf16[1152,2304]{1,0:T(8,128)(2,1)} %param.4), kind=kOutput, calls=%fused_computation.8 | convolution fusion | flops 16312762368 | bytes 23003136 | tf_op jit(solution)/shard_map/dot_general | solution.py:17
  72.3 1.6 collective-permute-start
  73.8 51.9 %collective-permute-done = f32[1152,512]{1,0:T(8,128)S(1)} collective-permute-done((f32[1152,512]{1,0:T(8,128)S(1)}, f32[1152,512]{1,0:T(8,128)S(1)}, u32[]{:S(2)}, u32[]{:S(2)}) %collective-permute-start) | collective-permute-done | bytes 2359328 | tf_op jit(solution)/shard_map/ppermute | solution.py:28
  126.3 2.5 collective-permute-start.1
  128.8 101.7 %collective-permute-done.1 = f32[1152,512]{1,0:T(8,128)} collective-permute-done((f32[1152,512]{1,0:T(8,128)S(1)}, f32[1152,512]{1,0:T(8,128)}, u32[]{:S(2)}, u32[]{:S(2)}) %collective-permute-start.1) | collective-permute-done | bytes 2359328 | tf_op jit(solution)/shard_map/ppermute | solution.py:28
  230.5 7.8 %fusion.16 = f32[512,512]{0,1:T(8,128)} fusion(f32[1152,512]{1,0:T(8,128)S(1)} %add.63, f32[1152,512]{1,0:T(8,128)} %collective-permute-done.1), kind=kOutput, calls=%fused_computation.31 | convolution fusion | flops 3624468480 | bytes 5767168 | tf_op jit(solution)/shard_map/dot_general | solution.py:17
  238.5 3.6 add_bitcast_fusion
  242.2 53.0 %all-reduce.4.cloned.1.call-done = f32[512,512]{0,1:T(8,128)} async-done(((f32[512,512]{0,1:T(8,128)}), f32[512,512]{0,1:T(8,128)}) %all-reduce.4.cloned.1.call-update) | async-done | bytes 1048592 | tf_op jit(solution)/shard_map/psum | solution.py:34
  295.1 1.6 copy.7
  297.0 11.7 %cholesky.104 = f32[128,128]{1,0:T(8,128)S(1)} custom-call(f32[128,128]{1,0:T(8,128)S(1)} %cholesky.266), custom_call_target="Cholesky" | custom-call | tf_op jit(solution)/shard_map/jit(cholesky)/cholesky | solution.py:12
  308.8 9.8 %custom-call.31 = f32[1,128,128]{1,2,0:T(8,128)S(1)} custom-call(f32[1,128,128]{2,1,0:T(8,128)S(1)} %get-tuple-element.30), custom_call_target="InvertDiagBlocksLowerTriangular" | custom-call | tf_op jit(solution)/shard_map/jit(cholesky)/cholesky | solution.py:12
  319.4 11.7 %cholesky.217 = f32[128,128]{1,0:T(8,128)S(1)} custom-call(f32[128,128]{1,0:T(8,128)S(1)} %cholesky.270), custom_call_target="Cholesky" | custom-call | tf_op jit(solution)/shard_map/jit(cholesky)/cholesky | solution.py:12
  331.1 10.2 %custom-call.32 = f32[1,128,128]{1,2,0:T(8,128)S(1)} custom-call(f32[1,128,128]{2,1,0:T(8,128)S(1)} %get-tuple-element.27), custom_call_target="InvertDiagBlocksLowerTriangular" | custom-call | tf_op jit(solution)/shard_map/jit(cholesky)/cholesky | solution.py:12
  342.0 11.7 %cholesky.238 = f32[128,128]{1,0:T(8,128)S(1)} custom-call(f32[128,128]{1,0:T(8,128)S(1)} %cholesky.275), custom_call_target="Cholesky" | custom-call | tf_op jit(solution)/shard_map/jit(cholesky)/cholesky | solution.py:12
  353.8 0.7 compare_reduce_fusion.1
  354.5 9.8 %custom-call.33 = f32[1,128,128]{1,2,0:T(8,128)S(1)} custom-call(f32[1,128,128]{2,1,0:T(8,128)S(1)} %get-tuple-element.24), custom_call_target="InvertDiagBlocksLowerTriangular" | custom-call | tf_op jit(solution)/shard_map/jit(cholesky)/cholesky | solution.py:12
  364.9 11.9 %cholesky.255 = f32[128,128]{1,0:T(8,128)S(1)} custom-call(f32[128,128]{1,0:T(8,128)S(1)} %convolution_subtract_fusion.2), custom_call_target="Cholesky" | custom-call | tf_op jit(solution)/shard_map/jit(cholesky)/cholesky | solution.py:12
  376.8 0.6 compare_reduce_fusion
  377.4 0.7 compare_reduce_fusion.2
  380.8 10.9 %while.1 = (s32[]{:T(128)}, f32[512,512]{1,0:T(8,128)S(1)}, s32[4,2]{0,1:T(2,128)S(1)}, f32[4,128,128]{2,1,0:T(8,128)}, s32[]{:T(128)}) while((s32[]{:T(128)}, f32[512,512]{1,0:T(8,128)S(1)}, s32[4,2]{0,1:T(2,128)S(1)}, f32[4,128,128]{2,1,0:T(8,128)}, s32[]{:T(128)}) %tuple.32), condition=%wide.while_cond, body=%wide.while_body.sunk | while | flops 2 | bytes 132205 | solution.py:13
  380.9 0.6 fusion.50
  381.5 2.1 bitcast_dynamic-update-slice_fusion.2
  383.6 0.6 fusion.50
  384.2 2.1 bitcast_dynamic-update-slice_fusion.2
  386.3 0.6 fusion.50
  386.9 2.1 bitcast_dynamic-update-slice_fusion.2
  389.1 0.6 fusion.50
  389.7 2.1 bitcast_dynamic-update-slice_fusion.2
  391.7 40.2 %custom-call.34 = f32[4,128,128]{1,2,0:T(8,128)S(1)} custom-call(f32[4,128,128]{2,1,0:T(8,128)} %get-tuple-element.10), custom_call_target="InvertDiagBlocksLowerTriangular" | custom-call | tf_op jit(solution)/shard_map/jit(_solve_triangular)/triangular_solve | solution.py:13
  431.9 1.9 fusion.21
  433.8 1.1 fusion.31
  434.9 1.9 fusion.20
  436.8 2.0 fusion.11
  438.9 0.7 fusion.19
  439.6 3.9 fusion.5
  443.5 0.7 fusion.18
  444.3 23.1 %fusion.2 = f32[512,2304]{1,0:T(8,128)} fusion(f32[1152,2304]{1,0:T(8,128)} %param.3, bf16[1152,2304]{1,0:T(8,128)(2,1)S(1)} %bitcast.51, f32[128,1152]{1,0:T(8,128)S(1)} %fusion.18, f32[128,1152]{1,0:T(8,128)S(1)} %fusion.19, f32[128,1152]{1,0:T(8,128)S(1)} %fusion.20, f32[128,1152]{1,0:T(8,128)S(1)} %fusion.21), kind=kOutput, calls=%fused_computation.7 | convolution fusion | flops 16314531840 | bytes 23003136 | tf_op jit(solution)/shard_map/dot_general | solution.py:17
  467.5 53.1 %reduce-scatter.2.cloned.1.call-done = f32[64,2304]{1,0:T(8,128)} async-done(((f32[512,2304]{1,0:T(8,128)}), f32[64,2304]{1,0:T(8,128)}) %reduce-scatter.2.cloned.1.call-update) | async-done | bytes 589840 | tf_op jit(solution)/shard_map/reduce_scatter | solution.py:37
  520.6 0.6 dynamic-slice.3
  521.8 1.2 multiply_reduce_fusion
  523.0 11.7 %psum.15 = f32[64]{0:T(128)S(1)} all-reduce(f32[64]{0:T(128)S(1)} %multiply_reduce_fusion), channel_id=1, replica_groups=mesh['wide'=8,'narrow'=4] {'narrow'}, use_global_device_ids=true, to_apply=%region_11.12 | all-reduce | flops 64 | bytes 512 | tf_op jit(solution)/shard_map/psum | solution.py:40
  534.8 12.1 %all-reduce.1 = f32[512]{0:T(512)S(1)} all-reduce(f32[512]{0:T(512)S(1)} %get-tuple-element.31), channel_id=1, replica_groups=mesh['wide'=8,'narrow'=4] {'wide'}, use_global_device_ids=true, to_apply=%add.1 | all-reduce | flops 512 | bytes 4096
  546.9 2.0 broadcast_divide_fusion
  548.9 12.3 %all-gather.5.cloned.1.call-done = f32[512,2304]{1,0:T(8,128)} async-done(((f32[64,2304]{1,0:T(8,128)}), f32[512,2304]{1,0:T(8,128)}) %all-gather.5.cloned.1.call-update) | async-done | bytes 4718608 | tf_op jit(solution)/shard_map/all_gather | solution.py:44
  561.3 24.1 %fusion = f32[1152,2304]{1,0:T(8,128)} fusion(f32[512,2304]{1,0:T(8,128)} %all-gather.5.cloned.1.call-done, f32[1152,2304]{1,0:T(8,128)} %param.3, bf16[1152,2304]{1,0:T(8,128)(2,1)} %param.4, f32[128,1152]{1,0:T(8,128)S(1)} %fusion.18, f32[128,1152]{1,0:T(8,128)S(1)} %fusion.19, f32[128,1152]{1,0:T(8,128)S(1)} %fusion.20, f32[128,1152]{1,0:T(8,128)S(1)} %fusion.21), kind=kOutput, calls=%fused_computation.3 | convolution fusion | flops 16319840256 | bytes 33619968 | tf_op jit(solution)/shard_map/dot_general | solution.py:17
  585.3 20.7 %convolution_convert_fusion = bf16[1152,2304]{1,0:T(8,128)(2,1)} fusion(f32[512,2304]{1,0:T(8,128)S(1)} %copy-done.1, f32[512]{0:T(512)S(1)} %all-reduce.1, f32[128,1152]{1,0:T(8,128)S(1)} %fusion.18, f32[128,1152]{1,0:T(8,128)S(1)} %fusion.19, f32[128,1152]{1,0:T(8,128)S(1)} %fusion.20, f32[128,1152]{1,0:T(8,128)S(1)} %fusion.21), kind=kOutput, calls=%fused_computation.4 | convolution fusion | flops 16313057280 | bytes 12388352 | tf_op jit(solution)/shard_map/dot_general | solution.py:17
  (52 shorter events, 3.9 us)
Async XLA Ops:
  7.2 44.2 %all-gather.3.cloned.1.call-start = ((), (), s32[]{:S(2)}) async-start(), calls=%async_computation.1 | async-start | bytes 5308416 | tf_op jit(solution)/shard_map/all_gather | solution.py:32
  7.9 287.2 %all-reduce.4.cloned.1.call-start = ((), (), s32[]{:S(2)}) async-start(), calls=%async_computation.2 | async-start | bytes 2097152 | tf_op jit(solution)/shard_map/psum | solution.py:34
  72.3 53.5 %collective-permute-start = (f32[1152,512]{1,0:T(8,128)S(1)}, f32[1152,512]{1,0:T(8,128)S(1)}, u32[]{:S(2)}, u32[]{:S(2)}) collective-permute-start(f32[1152,512]{1,0:T(8,128)S(1)} %fusion.3), channel_id=1, source_target_pairs={{0,1},{1,0},{2,3},{3,2},{4,5},{5,4},{6,7},{7,6},{8,9},{9,8},{10,11... | collective-permute-start | bytes 7077896 | tf_op jit(solution)/shard_map/ppermute | solution.py:28
  126.3 104.2 %collective-permute-start.1 = (f32[1152,512]{1,0:T(8,128)S(1)}, f32[1152,512]{1,0:T(8,128)}, u32[]{:S(2)}, u32[]{:S(2)}) collective-permute-start(f32[1152,512]{1,0:T(8,128)S(1)} %add.63), channel_id=1, source_target_pairs={{0,2},{1,3},{2,0},{3,1},{4,6},{5,7},{6,4},{7,5},{8,10},{9,11},{10,... | collective-permute-start | bytes 7077896 | tf_op jit(solution)/shard_map/ppermute | solution.py:28
  238.3 282.3 %reduce-scatter.2.cloned.1.call-start = ((), (), s32[]{:S(2)}) async-start(), calls=%async_computation.3 | async-start | bytes 5308416 | tf_op jit(solution)/shard_map/reduce_scatter | solution.py:37
  295.1 1.7 copy-start.2
  380.8 63.5 %slice-start = ((s8[5308416]{0:T(1024)(128)(4,1)}), s8[1114112]{0:T(1024)(128)(4,1)S(1)}, s32[]{:S(2)}) async-start(s8[5308416]{0:T(1024)(128)(4,1)} %bitcast.50), calls=%async_computation.5 | async-start | bytes 2228224
  391.7 45.1 %copy-start.3 = (f32[512,512]{1,0:T(8,128)}, f32[512,512]{1,0:T(8,128)S(1)}, u32[]{:S(2)}) copy-start(f32[512,512]{1,0:T(8,128)S(1)} %get-tuple-element.95) | copy-start | bytes 3145732
  431.9 1.9 copy-start.4
  433.8 5.1 copy-start
  434.9 3.9 copy-start.5
  436.8 7.5 %slice-start.1 = ((s8[5308416]{0:T(1024)(128)(4,1)}), s8[4194304]{0:T(1024)(128)(4,1)S(1)}, s32[]{:S(2)}) async-start(s8[5308416]{0:T(1024)(128)(4,1)} %bitcast.50), calls=%async_computation.6 | async-start | bytes 8388608
  467.4 53.2 %copy-start.6 = (u32[32]{0:T(128)S(1)}, u32[32]{0:T(128)}, u32[]{:S(2)}) copy-start(u32[32]{0:T(128)} %constant.172) | copy-start | bytes 388
  467.4 93.8 %all-gather.5.cloned.1.call-start = ((), (), s32[]{:S(2)}) async-start(), calls=%async_computation.4 | async-start | bytes 5308416 | tf_op jit(solution)/shard_map/all_gather | solution.py:44
  561.3 24.1 %copy-start.1 = (f32[512,2304]{1,0:T(8,128)S(1)}, f32[512,2304]{1,0:T(8,128)}, u32[]{:S(2)}) copy-start(f32[512,2304]{1,0:T(8,128)} %all-gather.5.cloned.1.call-done) | copy-start | bytes 14155780
Sparse Core Ops, SparseCore 0:
  9.9 41.4 all-gather.2
  238.4 56.6 all-reduce.3
  467.5 52.9 reduce-scatter.1
  522.3 38.9 all-gather.4
